TPU v7x, 32 devices: a whole 2x2x4 slice. The times are simulated.
32 devices in a mesh: chan: 2 (over x), vis: 2 (over core), pix: 8 (over z, y).
Axes of the slice: x: 2, y: 2, z: 4, core: 2. Of those that a mesh axis runs over, the one named last changes fastest.
Arguments:
- response: bfloat16 [16384, 49152], P(('chan', 'vis'), 'pix'), parts along dimension 0, may hold values from -5 to 5
- vis_data: float32 [16384], P(('chan', 'vis')), parts along dimension 0, may hold values from -6 to 6
- baseline_of_row: int32 [8192], P('vis'), may hold values from 0 to 8191
- noise_class: int32 [8192], P('vis'), may hold values from 0 to 15
- baseline_weight: float32 [8192], replicated, may hold values from 0.25 to 4
- class_inv_var: float32 [32], P('chan'), parts along dimension 0, may hold values from 0.25 to 4
Outputs:
- sky_map: float32 [98304], P(('chan', 'pix')), parts along dimension 0
- psf: float32 [98304, 64], P(('chan', 'pix'), 'vis'), parts along dimension 0
There are 2 independent parts, one for each index of `chan`. A program takes and returns all parts, laid end to end along the dimension named above; an argument that names none is the same for every part. Nothing has to cross between parts.
Inputs may be any that keep to these rules, and one draw needn't show every extreme that they name: `baseline_of_row`: baseline index of each row.
All inputs are finite; a program needn't handle non-finite values.
Results may differ from a plain program's by a relative error of at most 0.0041.
Values may be sent and summed in bfloat16 or wider, within the bound.
A program may use at most 128 MiB of HBM per device.

v0:
```python
import functools

import jax
import jax.numpy as jnp
from jax import lax
from jax.experimental import pallas as pl
from jax.experimental.pallas import tpu as pltpu
from jax.sharding import PartitionSpec as P

PANEL_DEV = 8
LANES = 128
EXTRA = 16
MESH_ID = pl.DeviceIdType.MESH
F32, BF16 = jnp.float32, jnp.bfloat16


def kernel(
    n_pix, n_early,
    resp, vis_h, base_h, cls_h, bw_h, civ_h,
    sky, psf,
    x, vis, base, cls, bw, civ, pbuf, w_ref, w2, lhs, nbuf, keep, sbuf, rbuf,
    qpart, qown, qrecv,
    in_sem, small_sem, psend, precv, vsend, vrecv, qsem,
):
    n_chunk, rows, ch = x.shape
    n_panel = n_pix * PANEL_DEV
    half = n_panel // 2
    me = lax.axis_index("pix")
    v = lax.axis_index("vis")
    other = 1 - v

    first = pltpu.make_async_copy(
        resp.at[:, pl.ds(0, LANES)], x.at[0, :, pl.ds(0, LANES)], in_sem.at[n_chunk]
    )
    first.start()
    smalls = [
        pltpu.make_async_copy(a, b, small_sem.at[i])
        for i, (a, b) in enumerate(
            [(vis_h, vis), (base_h, base), (cls_h, cls), (bw_h, bw), (civ_h, civ)]
        )
    ]
    for c in smalls:
        c.start()
    rest = None
    if ch > LANES:
        rest = pltpu.make_async_copy(
            resp.at[:, pl.ds(LANES, ch - LANES)],
            x.at[0, :, pl.ds(LANES, ch - LANES)],
            in_sem.at[0],
        )
        rest.start()

    def chunk_copy(c):
        return pltpu.make_async_copy(
            resp.at[:, pl.ds(pl.multiple_of(c * ch, ch), ch)], x.at[c], in_sem.at[c]
        )

    for c in range(1, n_chunk):
        chunk_copy(c).start()

    barrier = pltpu.get_barrier_semaphore()

    def greet(d, carry):
        pl.semaphore_signal(
            barrier, inc=1, device_id={"pix": lax.rem(me + d, n_pix)}, device_id_type=MESH_ID
        )
        return carry

    lax.fori_loop(1, n_pix, greet, 0)
    pl.semaphore_signal(barrier, inc=1, device_id={"vis": other}, device_id_type=MESH_ID)

    first.wait()
    pick = (
        lax.broadcasted_iota(jnp.int32, (16, LANES), 0)
        == lax.broadcasted_iota(jnp.int32, (16, LANES), 1)
    ).astype(BF16)
    own = lax.dot_general(
        pick, x[0, :, :LANES], (((1,), (1,)), ((), ())), preferred_element_type=F32
    )
    pbuf[me] = own[:PANEL_DEV].astype(BF16)
    pl.semaphore_wait(barrier, n_pix)

    def panel_copy(slot, peer):
        return pltpu.make_async_remote_copy(
            src_ref=pbuf.at[slot], dst_ref=pbuf.at[slot],
            send_sem=psend.at[peer], recv_sem=precv.at[slot],
            device_id={"pix": peer}, device_id_type=MESH_ID,
        )

    def send_panel(d, carry):
        panel_copy(me, lax.rem(me + d, n_pix)).start()
        return carry

    lax.fori_loop(1, n_pix, send_panel, 0)

    for c in smalls:
        c.wait()
    n_hi = bw.shape[0]
    t0 = bw[...].astype(BF16)
    left = bw[...] - t0.astype(F32)
    t1 = left.astype(BF16)
    t2 = (left - t1.astype(F32)).astype(BF16)
    table = jnp.concatenate([t0, t1, t2], axis=0)
    n_cls = civ.shape[1]
    diag = lax.broadcasted_iota(jnp.int32, (n_cls, n_cls), 0) == lax.broadcasted_iota(
        jnp.int32, (n_cls, n_cls), 1
    )
    civ_col = jnp.sum(
        jnp.where(diag, jnp.broadcast_to(civ[...], (n_cls, n_cls)), 0.0), axis=1, keepdims=True
    )
    step = min(rows, 512)

    def weights(i, carry):
        cols = pl.ds(pl.multiple_of(i * step, step), step)
        idx = base[:, cols]
        hi = lax.broadcast_in_dim(idx // LANES, (n_hi, step), (0, 1))
        lo = lax.broadcast_in_dim(lax.rem(idx, LANES), (LANES, step), (0, 1))
        hot = (hi == lax.broadcasted_iota(jnp.int32, (n_hi, step), 0)).astype(F32).astype(BF16)
        picked = lax.dot_general(
            table, jnp.concatenate([hot] * 3, axis=0), (((0,), (0,)), ((), ())),
            preferred_element_type=F32,
        )
        bw_row = jnp.sum(
            jnp.where(lo == lax.broadcasted_iota(jnp.int32, (LANES, step), 0), picked, 0.0),
            axis=0, keepdims=True,
        )
        kinds = lax.broadcast_in_dim(cls[:, cols], (n_cls, step), (0, 1))
        cw_row = jnp.sum(
            jnp.where(
                kinds == lax.broadcasted_iota(jnp.int32, (n_cls, step), 0), civ_col, 0.0
            ),
            axis=0, keepdims=True,
        )
        w = bw_row * cw_row
        w_ref[:, cols] = w
        w_hi = w.astype(BF16).astype(F32)
        at = lax.broadcasted_iota(jnp.int32, (EXTRA, step), 0)
        w2[:, cols] = jnp.where(
            at == 0, w_hi, jnp.where(at == 1, w - w_hi, 0.0)
        ).astype(BF16)
        lhs[n_panel:, cols] = jnp.where(at == 0, w * vis[:, cols], 0.0).astype(BF16)
        return carry

    lax.fori_loop(0, rows // step, weights, 0)

    kb = min(rows, 512)

    def norm_of(c):
        acc = None
        for k in range(0, rows, kb):
            xb = x[c, k : k + kb, :]
            part = jnp.dot(w2[:, k : k + kb], xb * xb, preferred_element_type=F32)
            acc = part if acc is None else acc + part
        nbuf[c] = jnp.broadcast_to(jnp.sum(acc, axis=0, keepdims=True), (8, ch))

    def vis_copy(c):
        return pltpu.make_async_remote_copy(
            src_ref=sbuf.at[c], dst_ref=rbuf.at[c],
            send_sem=vsend.at[c], recv_sem=vrecv.at[c],
            device_id={"vis": other}, device_id_type=MESH_ID,
        )

    def beam_of(c):
        res = jnp.dot(lhs[...], x[c], preferred_element_type=F32)
        at = lax.broadcasted_iota(jnp.int32, (8, ch), 0)
        pair = jnp.where(
            at == 0, res[n_panel : n_panel + 8], jnp.where(at == 1, nbuf[c], 0.0)
        )
        keep[c, :half] = res[:half]
        keep[c, half:] = pair
        sbuf[c, :half] = res[half:n_panel]
        sbuf[c, half:] = pair
        vis_copy(c).start()

    if rest is not None:
        rest.wait()
    norm_of(0)

    def early(c, carry):
        chunk_copy(c).wait()
        norm_of(c)
        return carry

    lax.fori_loop(1, n_early, early, 0)

    def wait_panel(d, carry):
        slot = lax.rem(me + d, n_pix)
        panel_copy(slot, slot).wait_recv()
        return carry

    lax.fori_loop(1, n_pix, wait_panel, 0)

    def weigh(j, carry):
        w = w_ref[...]
        src = lax.rem(2 * j + v * (n_pix // 2), n_pix)
        a = pbuf[src].astype(F32)
        b = pbuf[src + 1].astype(F32)
        wa, wb = w * a, w * b
        lhs[pl.ds(pl.multiple_of(j * 16, 16), 16), :] = jnp.concatenate([wa, wb], axis=0).astype(
            BF16
        )
        sq = jnp.concatenate(
            [
                jnp.sum(wa * a, axis=1, keepdims=True),
                jnp.sum(wb * b, axis=1, keepdims=True),
            ],
            axis=0,
        )
        qpart[pl.ds(pl.multiple_of(j * 16, 16), 16), :] = jnp.broadcast_to(sq, (16, LANES))
        return carry

    lax.fori_loop(0, n_pix // 2, weigh, 0)
    q_copy = pltpu.make_async_remote_copy(
        src_ref=qpart.at[pl.ds(half, half)], dst_ref=qrecv,
        send_sem=qsem.at[0], recv_sem=qsem.at[1],
        device_id={"vis": other}, device_id_type=MESH_ID,
    )
    q_copy.start()

    def backlog(c, carry):
        beam_of(c)
        return carry

    lax.fori_loop(0, n_early, backlog, 0)

    q_copy.wait()
    qown[...] = lax.rsqrt(qpart[:half, :1] + qrecv[:, :1]) * jnp.ones((1, LANES), F32)

    def final(c, carry):
        vis_copy(c).wait_recv()
        cols = pl.ds(pl.multiple_of(c * ch, ch), ch)
        pair = keep[c, half:] + rbuf[c, half:]
        scale = lax.rsqrt(pair[1:2])
        sky[:, cols] = pair[0:1] * scale
        psf[:, cols] = (keep[c, :half] + rbuf[c, :half]) * scale * qown[:, :1]
        return carry

    lax.fori_loop(0, n_early, final, 0)

    def late(c, carry):
        chunk_copy(c).wait()
        norm_of(c)
        beam_of(c)

        @pl.when(c > n_early)
        def _():
            final(c - 1, 0)

        return carry

    lax.fori_loop(n_early, n_chunk, late, 0)
    final(n_chunk - 1, 0)

    def drain(c, carry):
        vis_copy(c).wait_send()
        return carry

    lax.fori_loop(0, n_chunk, drain, 0)

    def drain_panel(d, carry):
        panel_copy(me, lax.rem(me + d, n_pix)).wait_send()
        return carry

    lax.fori_loop(1, n_pix, drain_panel, 0)


def shards(n_pix, response, vis_data, baseline_of_row, noise_class, baseline_weight, class_inv_var):
    rows, pix = response.shape
    ch = next(c for c in (1024, 768, 512, 256, 128) if pix % c == 0)
    n_chunk = pix // ch
    n_early = max(1, n_chunk // 3)
    n_panel = n_pix * PANEL_DEV
    half = n_panel // 2
    n_hi = baseline_weight.shape[0] // LANES
    n_cls = class_inv_var.shape[0]
    vmem, dma = pltpu.VMEM, pltpu.SemaphoreType.DMA
    sky, psf = pl.pallas_call(
        functools.partial(kernel, n_pix, n_early),
        out_shape=(
            pltpu.VMEM((1, pix), F32),
            pltpu.VMEM((half, pix), F32),
        ),
        in_specs=[pl.BlockSpec(memory_space=pltpu.HBM)] * 6,
        out_specs=(pl.BlockSpec(memory_space=pltpu.VMEM),) * 2,
        scratch_shapes=[
            vmem((n_chunk, rows, ch), BF16),
            vmem((1, rows), F32),
            vmem((1, rows), jnp.int32),
            vmem((1, rows), jnp.int32),
            vmem((n_hi, LANES), F32),
            vmem((1, n_cls), F32),
            vmem((n_pix, PANEL_DEV, rows), BF16),
            vmem((1, rows), F32),
            vmem((EXTRA, rows), BF16),
            vmem((n_panel + EXTRA, rows), BF16),
            vmem((n_chunk, 8, ch), F32),
            vmem((n_chunk, half + 8, ch), F32),
            vmem((n_chunk, half + 8, ch), F32),
            vmem((n_chunk, half + 8, ch), F32),
            vmem((n_panel, LANES), F32),
            vmem((half, LANES), F32),
            vmem((half, LANES), F32),
            dma((n_chunk + 1,)),
            dma((5,)),
            dma((n_pix,)),
            dma((n_pix,)),
            dma((n_chunk,)),
            dma((n_chunk,)),
            dma((2,)),
        ],
        compiler_params=pltpu.CompilerParams(
            collective_id=0, has_side_effects=True, vmem_limit_bytes=58 * 1024 * 1024
        ),
    )(
        response,
        vis_data.reshape(1, rows),
        baseline_of_row.reshape(1, rows),
        noise_class.reshape(1, rows),
        baseline_weight.reshape(n_hi, LANES),
        class_inv_var.reshape(1, n_cls),
    )
    return sky.reshape(pix), psf.T


def solution(mesh):
    placed = (P(("chan", "vis"), "pix"), P(("chan", "vis")), P("vis"), P("vis"), P(), P("chan"))
    return jax.shard_map(
        functools.partial(shards, mesh.shape["pix"]),
        mesh=mesh,
        in_specs=placed,
        out_specs=(P(("chan", "pix")), P(("chan", "pix"), "vis")),
        check_vma=False,
    )
```

profile of v0, /device:TPU:0, one launch (start us, length us, event | category | flops | bytes accessed | tf_op | source)
XLA Modules:
  0.0 37.1 jit_solution(501479164981112291)
XLA Ops:
  0.6 35.0 %shard_map.77 = (f32[1,6144]{1,0:T(1,128)S(1)}, f32[32,6144]{1,0:T(8,128)S(1)}) custom-call(bf16[4096,6144]{1,0:T(8,128)(2,1)} %resp.1, f32[1,4096]{1,0:T(1,128)} %bitcast.10, s32[1,4096]{1,0:T(1,128)} %bitcast.11, s32[1,4096]{1,0:T(1,128)} %bitcast.12, f32[64,128]{1,0:T(8,128)} %bitcast.9, f32[1,16]{1,0:T(1,128)} %bitcast.13), custom_call_target="tpu_custom_call" | custom-call | tf_op jit(solution)/shard_map/pallas_call | solution.py:277
  35.6 0.6 %copy.10 = f32[6144]{0:T(1024)} copy(f32[6144]{0:T(1024)S(1)} %bitcast.8) | data formatting | bytes 49152
  36.2 0.9 %copy.11 = f32[6144,32]{0,1:T(8,128)} copy(f32[6144,32]{0,1:T(8,128)S(1)} %bitcast.7) | data formatting | bytes 1572864
where the time goes:
time: 37.4 us; the launch traced here: 37.1 us
  Pallas kernels  35 us (94%)
  local copies, waits for them, and re-layouts  1.49 us (4%)
  between operations  0.64 us (2%)
    pallas_call x1, Pallas kernels, shards(): pl.pallas_call(functools.partial(kernel, n_pix, n_early), out_shape=(pltp...  35 us
    unnamed x2, local copies, waits for them, and re-layouts  1.49 us

commit v1 on v0

v1 whole, which is shorter than its diff:
```python
import functools

import jax
import jax.numpy as jnp
from jax import lax
from jax.experimental import pallas as pl
from jax.experimental.pallas import tpu as pltpu
from jax.sharding import PartitionSpec as P

PANEL_DEV = 8
LANES = 128
TILE = 256
EXTRA = 16
MESH_ID = pl.DeviceIdType.MESH
F32, BF16 = jnp.float32, jnp.bfloat16


def kernel(
    n_pix, n_in, n_block, ch,
    resp, vis_h, base_h, cls_h, bw_h, civ_h,
    sky, psf,
    x, vis, base, cls, bw, civ, pbuf, w_ref, wcol, lhs, nacc, acc, rbuf,
    qbuf, qown, qrecv,
    in_sem, small_sem, psend, precv, vsend, vrecv, qsem,
):
    rows, pix = x.shape
    rb = rows // n_block
    n_panel = n_pix * PANEL_DEV
    half = n_panel // 2
    me = lax.axis_index("pix")
    v = lax.axis_index("vis")
    other = 1 - v
    n_out = n_pix // n_in
    zi, yi = me // n_in, lax.rem(me, n_in)

    def slot_of(source):
        return lax.rem(source + v * (n_pix // 2), n_pix)

    def line(d):
        return lax.rem(zi + d, n_out) * n_in + yi

    def side(d):
        return zi * n_in + lax.rem(yi + d, n_in)

    home = slot_of(me)

    smalls = [
        pltpu.make_async_copy(a, b, small_sem.at[i])
        for i, (a, b) in enumerate(
            [(base_h, base), (bw_h, bw), (cls_h, cls), (civ_h, civ), (vis_h, vis)]
        )
    ]
    for c in smalls:
        c.start()
    first = pltpu.make_async_copy(
        resp.at[:, pl.ds(0, LANES)], x.at[:, pl.ds(0, LANES)], small_sem.at[5]
    )
    first.start()

    def piece(r, c):
        lo = LANES if c == 0 else c * ch
        at = (pl.ds(r * rb, rb), pl.ds(lo, (c + 1) * ch - lo))
        return pltpu.make_async_copy(resp.at[at], x.at[at], in_sem.at[r, c])

    def has_piece(c):
        return ch > LANES or c > 0

    for r in range(n_block):
        for c in range(pix // ch):
            if has_piece(c):
                piece(r, c).start(priority=1)

    barrier = pltpu.get_barrier_semaphore()

    for d in range(1, n_out):
        pl.semaphore_signal(
            barrier, inc=1, device_id={"pix": line(d)}, device_id_type=MESH_ID
        )
    for d in range(1, n_in):
        pl.semaphore_signal(
            barrier, inc=1, device_id={"pix": side(d)}, device_id_type=MESH_ID
        )
    pl.semaphore_signal(barrier, inc=1, device_id={"vis": other}, device_id_type=MESH_ID)

    for c in smalls:
        c.wait()
    n_hi = bw.shape[0]
    t0 = bw[...].astype(BF16)
    left = bw[...] - t0.astype(F32)
    t1 = left.astype(BF16)
    t2 = (left - t1.astype(F32)).astype(BF16)
    table = jnp.concatenate([t0, t1, t2], axis=0)
    n_cls = civ.shape[1]
    diag = lax.broadcasted_iota(jnp.int32, (n_cls, n_cls), 0) == lax.broadcasted_iota(
        jnp.int32, (n_cls, n_cls), 1
    )
    civ_col = jnp.sum(
        jnp.where(diag, jnp.broadcast_to(civ[...], (n_cls, n_cls)), 0.0), axis=1, keepdims=True
    )
    step = min(rows, 512)
    with jax.named_scope("weights"):
        for i in range(rows // step):
            cols = pl.ds(i * step, step)
            idx = base[:, cols]
            hi = lax.broadcast_in_dim(idx // LANES, (n_hi, step), (0, 1))
            lo = lax.broadcast_in_dim(lax.rem(idx, LANES), (LANES, step), (0, 1))
            hot = (hi == lax.broadcasted_iota(jnp.int32, (n_hi, step), 0)).astype(F32).astype(BF16)
            picked = lax.dot_general(
                table, jnp.concatenate([hot] * 3, axis=0), (((0,), (0,)), ((), ())),
                preferred_element_type=F32,
            )
            bw_row = jnp.sum(
                jnp.where(lo == lax.broadcasted_iota(jnp.int32, (LANES, step), 0), picked, 0.0),
                axis=0, keepdims=True,
            )
            kinds = lax.broadcast_in_dim(cls[:, cols], (n_cls, step), (0, 1))
            cw_row = jnp.sum(
                jnp.where(
                    kinds == lax.broadcasted_iota(jnp.int32, (n_cls, step), 0), civ_col, 0.0
                ),
                axis=0, keepdims=True,
            )
            w_ref[:, cols] = jnp.broadcast_to(bw_row * cw_row, (PANEL_DEV, step))

    with jax.named_scope("panel"):
        first.wait()
        pick = (
            lax.broadcasted_iota(jnp.int32, (16, LANES), 0)
            == lax.broadcasted_iota(jnp.int32, (16, LANES), 1)
        ).astype(BF16)
        sums = jnp.zeros((PANEL_DEV, 1), F32)
        for r in range(n_block):
            at = pl.ds(r * rb, rb)
            own = lax.dot_general(
                pick, x[at, :LANES], (((1,), (1,)), ((), ())), preferred_element_type=F32
            )[:PANEL_DEV]
            weighted = own * w_ref[:, at]
            sums = sums + jnp.sum(weighted * own, axis=1, keepdims=True)
            pbuf[r, home] = weighted.astype(BF16)
        qbuf[home] = jnp.broadcast_to(sums, (PANEL_DEV, LANES))

    with jax.named_scope("barrier"):
        pl.semaphore_wait(barrier, n_out + n_in - 1)

    def panel_copy(r, source, peer, i):
        slot = slot_of(source)
        if r == n_block:
            return pltpu.make_async_remote_copy(
                src_ref=qbuf.at[slot], dst_ref=qbuf.at[slot],
                send_sem=psend.at[r, i], recv_sem=precv.at[r, slot],
                device_id={"pix": peer}, device_id_type=MESH_ID,
            )
        return pltpu.make_async_remote_copy(
            src_ref=pbuf.at[r, slot], dst_ref=pbuf.at[r, slot],
            send_sem=psend.at[r, i], recv_sem=precv.at[r, slot],
            device_id={"pix": peer}, device_id_type=MESH_ID,
        )

    def own_copies(r):
        out = [panel_copy(r, me, line(d), d - 1) for d in range(n_out - 1, 0, -1)]
        return out + [panel_copy(r, me, side(d), n_out + d - 2) for d in range(1, n_in)]

    def relay(r, d, e):
        return panel_copy(r, line(d), side(e), n_out + n_in - 2 + (d - 1) * (n_in - 1) + e - 1)

    for r in range(n_block + 1):
        for c in own_copies(r):
            c.start()

    def forward(r):
        with jax.named_scope("forward%d" % r):
            for d in range(1, n_out):
                panel_copy(r, line(d), me, 0).wait_recv()
                for e in range(1, n_in):
                    relay(r, d, e).start()

    with jax.named_scope("wcol"):
        at = lax.broadcasted_iota(jnp.int32, (EXTRA, rb), 0)
        unit = (lax.broadcasted_iota(jnp.int32, (EXTRA, LANES), 0) == 0).astype(BF16)
        for r in range(n_block):
            cols = pl.ds(r * rb, rb)
            w = jnp.concatenate([w_ref[:, cols]] * 2, axis=0)
            lhs[n_panel : n_panel + EXTRA, cols] = jnp.where(at == 0, w * vis[:, cols], 0.0).astype(BF16)
            wcol[cols, :] = lax.dot_general(
                w.astype(BF16), unit, (((0,), (0,)), ((), ())), preferred_element_type=F32
            ).astype(BF16)

    fold = rb // TILE if rb % TILE == 0 else 1
    kb = rb // fold
    ones = jnp.ones((16, kb), BF16)
    pad = lhs.shape[0] - n_panel - EXTRA
    if pad:
        lhs[n_panel + EXTRA :, :] = jnp.zeros((pad, rows), BF16)

    def norm_part(r, lo, n):
        parts = []
        wide = TILE if n % TILE == 0 else LANES
        for s in range(lo, lo + n, wide):
            total = None
            for i in range(fold):
                at = pl.ds(r * rb + i * kb, kb)
                xb = x[at, pl.ds(s, wide)]
                term = xb * xb * jnp.concatenate([wcol[at, :]] * (wide // LANES), axis=1)
                total = term if total is None else total + term
            parts.append(jnp.dot(ones, total, preferred_element_type=F32)[:8])
        return jnp.concatenate(parts, axis=1) if len(parts) > 1 else parts[0]

    def norm_step(r, c):
        wait_x(r, c)
        cols = pl.ds(c * ch, ch)
        got = norm_part(r, c * ch, ch)
        nacc[:, cols] = got if r == 0 else nacc[:, cols] + got

    def beam_part(r, lo, n):
        cols = pl.ds(lo, n)
        return jnp.dot(
            lhs[:, r * rb : (r + 1) * rb], x[r * rb : (r + 1) * rb, cols],
            preferred_element_type=F32,
        )[: n_panel + 8]

    sub = next(s for s in (512, 384, 256, 128) if ch % s == 0)

    def beam_step(r, c):
        for lo in range(c * ch, (c + 1) * ch, sub):
            got = beam_part(r, lo, sub)
            cols = pl.ds(lo, sub)
            acc[:, cols] = got if r == 0 else acc[:, cols] + got

    def wait_x(r, c):
        if has_piece(c):
            piece(r, c).wait()

    def others(r):
        def one(i, carry):
            d, e = i // (n_in - 1), lax.rem(i, n_in - 1) + 1
            source = lax.rem(zi + d, n_out) * n_in + lax.rem(yi + e, n_in)
            panel_copy(r, source, me, 0).wait_recv()
            return carry

        lax.fori_loop(0, n_out * (n_in - 1), one, 0)

    def panel(r):
        with jax.named_scope("panel%d" % r):
            others(r)
            cols = pl.ds(r * rb, rb)
            for j in range(n_pix // 2):
                lhs[16 * j : 16 * j + 16, cols] = jnp.concatenate(
                    [pbuf[r, 2 * j], pbuf[r, 2 * j + 1]], axis=0
                )

    wide = pix // ch
    last = n_block - 1
    todo = []
    if n_block == 4:
        todo += [("A", 0, c) for c in range(wide)]
        todo += [("A", 1, c) for c in range(wide - 1)] + [("F", 0, 0)]
        todo += [("A", 1, wide - 1), ("F", 1, 0), ("A", 2, 0), ("F", 2, 0)]
        todo += [("A", 2, c) for c in range(1, wide)]
        todo += [("P", 0, 0)] + [("B", 0, c) for c in range(wide)]
        todo += [("F", 3, 0), ("F", 4, 0), ("P", 1, 0), ("A", 3, 0)] + [("B", 1, c) for c in range(wide)]
        todo += [("P", 2, 0)] + [("A", 3, c) for c in range(1, wide)] + [("B", 2, c) for c in range(wide)]
    else:
        for r in range(n_block):
            todo += [("A", r, c) for c in range(wide)]
        todo += [("F", r, 0) for r in range(n_block + 1)]
        for r in range(last):
            todo += [("P", r, 0)] + [("B", r, c) for c in range(wide)]
    for kind, r, c in todo:
        if kind == "F":
            forward(r)
        elif kind == "P":
            panel(r)
        else:
            with jax.named_scope("%s%d_%d" % (kind, r, c)):
                {"A": norm_step, "B": beam_step}[kind](r, c)
    panel(last)

    with jax.named_scope("qwait"):
        others(n_block)
    q_copy = pltpu.make_async_remote_copy(
        src_ref=qbuf.at[pl.ds(n_pix // 2, n_pix // 2)], dst_ref=qrecv,
        send_sem=qsem.at[0], recv_sem=qsem.at[1],
        device_id={"vis": other}, device_id_type=MESH_ID,
    )
    q_copy.start()

    spans = [(c * ch, ch) for c in range(wide)]
    while len(spans) < wide + 2 and spans[-1][1] % (2 * sub) == 0:
        lo, n = spans.pop()
        spans += [(lo, n // 2), (lo + n // 2, n // 2)]

    def vis_copy(i):
        cols = pl.ds(*spans[i])
        return pltpu.make_async_remote_copy(
            src_ref=acc.at[pl.ds(half, half + 8), cols], dst_ref=rbuf.at[:, cols],
            send_sem=vsend.at[i], recv_sem=vrecv.at[i],
            device_id={"vis": other}, device_id_type=MESH_ID,
        )

    def last_step(i):
        for lo in range(spans[i][0], sum(spans[i]), sub):
            cols = pl.ds(lo, sub)
            got = beam_part(last, lo, sub)
            if last > 0:
                got = got + acc[:, cols]
            at = lax.broadcasted_iota(jnp.int32, (8, sub), 0)
            acc[:n_panel, cols] = got[:n_panel]
            acc[n_panel:, cols] = jnp.where(at == 1, nacc[:, cols], got[n_panel:])
        vis_copy(i).start()

    def final(i):
        vis_copy(i).wait_recv()
        for lo in range(spans[i][0], sum(spans[i]), sub):
            cols = pl.ds(lo, sub)
            pair = acc[n_panel:, cols] + rbuf[half:, cols]
            scale = lax.rsqrt(pair[1:2])
            sky[:, cols] = pair[0:1] * scale
            psf[:, cols] = (acc[:half, cols] + rbuf[:half, cols]) * scale * qown[:, :1]

    lag = 2
    for i in range(len(spans) + lag):
        if i < len(spans):
            with jax.named_scope("L%d" % i):
                last_step(i)
        if i == lag:
            with jax.named_scope("qcopy"):
                q_copy.wait()
                mine = qbuf[: n_pix // 2].reshape(half, LANES)
                qown[...] = lax.rsqrt(mine + qrecv[...].reshape(half, LANES))
        if 0 <= i - lag < len(spans):
            with jax.named_scope("final%d" % (i - lag)):
                final(i - lag)

    for i in range(len(spans)):
        vis_copy(i).wait_send()
    for r in range(n_block + 1):
        for c in own_copies(r):
            c.wait_send()
        for d in range(1, n_out):
            for e in range(1, n_in):
                relay(r, d, e).wait_send()


def shards(n_pix, response, vis_data, baseline_of_row, noise_class, baseline_weight, class_inv_var):
    rows, pix = response.shape
    ch = next(c for c in (2048, 1536, 1024, 768, 512, 384, 256, 128) if pix % c == 0)
    n_in = max(d for d in range(1, n_pix + 1) if n_pix % d == 0 and d * d <= n_pix)
    n_block = next(b for b in (4, 2, 1) if rows % (b * 256) == 0 or b == 1)
    n_panel = n_pix * PANEL_DEV
    half = n_panel // 2
    n_hi = baseline_weight.shape[0] // LANES
    n_cls = class_inv_var.shape[0]
    vmem, dma = pltpu.VMEM, pltpu.SemaphoreType.DMA
    sky, psf = pl.pallas_call(
        functools.partial(kernel, n_pix, n_in, n_block, ch),
        out_shape=(
            pltpu.VMEM((1, pix), F32),
            pltpu.VMEM((half, pix), F32),
        ),
        in_specs=[pl.BlockSpec(memory_space=pltpu.HBM)] * 6,
        out_specs=(pl.BlockSpec(memory_space=pltpu.VMEM),) * 2,
        scratch_shapes=[
            vmem((rows, pix), BF16),
            vmem((1, rows), F32),
            vmem((1, rows), jnp.int32),
            vmem((1, rows), jnp.int32),
            vmem((n_hi, LANES), F32),
            vmem((1, n_cls), F32),
            vmem((n_block, n_pix, PANEL_DEV, rows // n_block), BF16),
            vmem((PANEL_DEV, rows), F32),
            vmem((rows, LANES), BF16),
            vmem((max(n_panel + EXTRA, LANES), rows), BF16),
            vmem((8, pix), F32),
            vmem((n_panel + 8, pix), F32),
            vmem((half + 8, pix), F32),
            vmem((n_pix, PANEL_DEV, LANES), F32),
            vmem((half, LANES), F32),
            vmem((n_pix // 2, PANEL_DEV, LANES), F32),
            dma((n_block, pix // ch)),
            dma((6,)),
            dma((n_block + 1, 2 * n_pix)),
            dma((n_block + 1, n_pix)),
            dma((pix // ch + 2,)),
            dma((pix // ch + 2,)),
            dma((2,)),
        ],
        compiler_params=pltpu.CompilerParams(
            collective_id=0, has_side_effects=True, vmem_limit_bytes=60 * 1024 * 1024
        ),
    )(
        response,
        vis_data.reshape(1, rows),
        baseline_of_row.reshape(1, rows),
        noise_class.reshape(1, rows),
        baseline_weight.reshape(n_hi, LANES),
        class_inv_var.reshape(1, n_cls),
    )
    return sky.reshape(pix), psf.T


def solution(mesh):
    placed = (P(("chan", "vis"), "pix"), P(("chan", "vis")), P("vis"), P("vis"), P(), P("chan"))
    return jax.shard_map(
        functools.partial(shards, mesh.shape["pix"]),
        mesh=mesh,
        in_specs=placed,
        out_specs=(P(("chan", "pix")), P(("chan", "pix"), "vis")),
        check_vma=False,
    )
```

time: 37.4 us -> 28.6 us (0.76)
  Pallas kernels: 35 us -> 26.2 us
    pallas_call x1, Pallas kernels: 35 us -> 26.2 us  [shards(): pl.pallas_call(functools.partial(kernel, n_pix, n_in, n_block, ch), out_s...]
where the time goes in v1:
time: 28.6 us; the launch traced here: 28.3 us
  Pallas kernels  26.2 us (92%)
  local copies, waits for them, and re-layouts  1.49 us (5%)
  between operations  0.64 us (2%)
    pallas_call x1, Pallas kernels, shards(): pl.pallas_call(functools.partial(kernel, n_pix, n_in, n_block, ch), out_s...  26.2 us
    unnamed x2, local copies, waits for them, and re-layouts  1.49 us

profile of v1, /device:TPU:0, one launch (start us, length us, event | category | flops | bytes accessed | tf_op | source)
XLA Modules:
  0.0 28.3 jit_solution(11288837687919673680)
XLA Ops:
  0.6 26.2 %shard_map.77 = (f32[1,6144]{1,0:T(1,128)S(1)}, f32[32,6144]{1,0:T(8,128)S(1)}) custom-call(bf16[4096,6144]{1,0:T(8,128)(2,1)} %resp.1, f32[1,4096]{1,0:T(1,128)} %bitcast.10, s32[1,4096]{1,0:T(1,128)} %bitcast.11, s32[1,4096]{1,0:T(1,128)} %bitcast.12, f32[64,128]{1,0:T(8,128)} %bitcast.9, f32[1,16]{1,0:T(1,128)} %bitcast.13), custom_call_target="tpu_custom_call" | custom-call | tf_op jit(solution)/shard_map/pallas_call | solution.py:354
  26.8 0.6 %copy.10 = f32[6144]{0:T(1024)} copy(f32[6144]{0:T(1024)S(1)} %bitcast.8) | data formatting | bytes 49152
  27.5 0.9 %copy.11 = f32[6144,32]{0,1:T(8,128)} copy(f32[6144,32]{0,1:T(8,128)S(1)} %bitcast.7) | data formatting | bytes 1572864
